TPU v7x, 32 devices: a whole 2x2x4 slice. The times are simulated.
32 devices in a mesh: groups: 2 (over x), blk: 8 (over z, y), span: 2 (over core).
Axes of the slice: x: 2, y: 2, z: 4, core: 2. Of those that a mesh axis runs over, the one named last changes fastest.
Arguments:
- embeddings: bfloat16 [8192, 768], P(('groups', 'blk', 'span')), parts along dimension 0, may hold values from -6 to 6
- owner_ids: int32 [8192, 1], P(('groups', 'blk', 'span')), parts along dimension 0, may hold values from 0 to 7, as said below
- local_ids: int32 [8192], P(('groups', 'blk', 'span')), parts along dimension 0, may hold values from 0 to 15, as said below
- cluster_map: int32 [256], P('groups'), parts along dimension 0, may hold values from 0 to 127, as said below
Outputs:
- nearest: float32 [8192], P(('groups', 'blk', 'span')), parts along dimension 0
- centroid_cosine: float32 [8192], P(('groups', 'blk', 'span')), parts along dimension 0
There are 2 independent parts, one for each index of `groups`. A program takes and returns all parts, laid end to end along the dimension named above; each array names one. Nothing has to cross between parts.
Inputs may be any that keep to these rules, and one draw needn't show every extreme that they name: `owner_ids`: at most 64 rows of one device name the same owner; in every draw one owner is named by exactly 64 rows of every device. `local_ids`: of the rows of one device that name one owner, at most 16 have local id 0; in every draw one owner receives exactly 16 rows with local id 0 from every device. In every draw some clusters with a local id other than 0 have exactly one row in the whole shard. cluster_map[o * 16 + l] = o * 16 + l for l > 0. For l = 0 the owners fall into runs of 1 to 3 consecutive owners, and every owner of a run has the value of the run's first owner; some run has 3 owners.
All inputs are finite; a program needn't handle non-finite values.
Results may differ from a plain program's by a relative error of at most 0.0017.
Values may be sent and summed in bfloat16 or wider, within the bound.
No kernel may reach another device: no remote copies, remote signals or barrier semaphores. Data moves between devices by JAX's collectives and lax.ppermute only.
A program may use at most 64 MiB of HBM per device.

v0:
```python
import jax
import jax.numpy as jnp
from jax import lax
from jax.sharding import PartitionSpec as P

GIANT_SPAN = 3


def passed_along(value, axis, steps):
    count = lax.axis_size(axis)
    first, last = (max(0, -steps), min(count, count - steps))
    return lax.ppermute(value, axis, [(source, source + steps) for source in range(first, last)])


def normalize(values):
    wide = values.astype(jnp.float32)
    scale = lax.rsqrt(jnp.sum(wide * wide, axis=1, keepdims=True) + 1e-06)
    return (wide * scale).astype(jnp.bfloat16)


def masked_scores(left, left_tags, right, right_tags):
    scores = lax.dot_general(
        left, right, (((1,), (1,)), ((), ())), preferred_element_type=jnp.float32
    )
    same = (left_tags[:, None] == right_tags[None, :]) & (left_tags[:, None] > 0)
    return jnp.where(same, scores, -1.0)


def body(embeddings, owner_ids, local_ids, cluster_map):
    rows = embeddings.shape[0]
    width = embeddings.shape[1]
    owners = lax.axis_size("blk")
    capacity = 2 * rows // owners
    slots = owners * capacity
    clusters = cluster_map.shape[0]
    owned = clusters // owners
    unit = normalize(embeddings)
    destination = owner_ids[:, 0]
    flat = destination * owned + local_ids
    table = jnp.arange(clusters, dtype=jnp.int32)
    cluster = jnp.sum(jnp.where(flat[:, None] == table[None, :], cluster_map[None, :], 0), axis=1)
    onehot = (destination[:, None] == jnp.arange(owners, dtype=jnp.int32)[None, :]).astype(
        jnp.int32
    )
    before = jnp.cumsum(onehot, axis=0) - onehot
    rank = jnp.sum(before * onehot, axis=1)
    position = destination * capacity + rank
    send_rows = jnp.zeros((slots, width), jnp.bfloat16).at[position].set(unit)
    send_tags = jnp.zeros((slots,), jnp.int32).at[position].set(cluster + 1)
    arrived, arrived_tags = (
        lax.all_to_all(
            send_rows.reshape(owners, capacity, width),
            "blk",
            split_axis=0,
            concat_axis=0,
            tiled=True,
        ),
        lax.all_to_all(
            send_tags.reshape(owners, capacity), "blk", split_axis=0, concat_axis=0, tiled=True
        ),
    )
    mine = arrived.reshape(slots, width)
    my_tags = arrived_tags.reshape(slots)
    chip, chip_tags = (
        lax.all_gather(mine, "span", axis=0, tiled=True),
        lax.all_gather(my_tags, "span", axis=0, tiled=True),
    )
    half = lax.axis_index("span")
    block_index = lax.axis_index("blk")
    own_tags = lax.dynamic_slice_in_dim(cluster_map, block_index * owned, owned, 0) + 1
    local = masked_scores(mine, my_tags, chip, chip_tags)
    itself = (
        jnp.arange(2 * slots, dtype=jnp.int32)[None, :]
        == (jnp.arange(slots, dtype=jnp.int32) + half * slots)[:, None]
    )
    best = jnp.max(jnp.where(itself, -1.0, local), axis=1)
    share_limit = 2 * owners * max(1, capacity // 4)
    shared_mask = chip_tags == own_tags[0]
    packed_rank = jnp.cumsum(shared_mask.astype(jnp.int32)) - 1
    target = jnp.where(shared_mask, packed_rank, share_limit)
    packed = jnp.zeros((share_limit, width), jnp.bfloat16).at[target].set(chip, mode="drop")
    packed_tags = jnp.zeros((share_limit,), jnp.int32).at[target].set(chip_tags, mode="drop")
    upper = (packed, packed_tags)
    lower = (packed, packed_tags)
    for step in range(1, GIANT_SPAN):
        upper = passed_along((upper[0], upper[1]), "blk", 1)
        lower = passed_along((lower[0], lower[1]), "blk", -1)
        for other in (upper, lower):
            best = jnp.maximum(
                best, jnp.max(masked_scores(mine, my_tags, other[0], other[1]), axis=1)
            )
    chosen = cluster[:, None] == table[None, :]
    partial_sums = lax.dot_general(
        chosen.astype(jnp.bfloat16),
        unit,
        (((0,), (0,)), ((), ())),
        preferred_element_type=jnp.float32,
    )
    sums = lax.psum(partial_sums, ("blk", "span"))
    length = jnp.sqrt(jnp.sum(sums * sums, axis=1, keepdims=True))
    direction = sums / jnp.maximum(length, 1.0)
    centroid_cosine = jnp.sum(unit.astype(jnp.float32) * direction[cluster], axis=1)
    returned_best = lax.all_to_all(
        best.reshape(owners, capacity), "blk", split_axis=0, concat_axis=0, tiled=True
    )
    nearest = returned_best.reshape(slots)[position]
    return (nearest, centroid_cosine)


def solution(mesh):
    return jax.shard_map(
        body,
        mesh=mesh,
        in_specs=(
            P(("groups", "blk", "span"), None),
            P(("groups", "blk", "span"), None),
            P(("groups", "blk", "span")),
            P("groups"),
        ),
        out_specs=(P(("groups", "blk", "span")), P(("groups", "blk", "span"))),
        check_vma=False,
    )
```

profile of v0, /device:TPU:0, one launch (start us, length us, event | category | flops | bytes accessed | tf_op | source)
XLA Modules:
  0.0 191.0 jit_solution(9322189716579336675)
XLA Ops:
  12.2 3.1 %scatter_custom_fusion.1 = bf16[512,768]{1,0:T(8,128)(2,1)} fusion(s32[256]{0:T(256)S(1)} %bitcast.54, bf16[]{:T(256)} %constant.23.clone.1, bf16[256,768]{1,0:T(8,128)(2,1)} %param.4, f32[256]{0:T(256)S(1)} %add_rsqrt_fusion), kind=kCustom, calls=%fused_computation.18 | custom fusion | flops 589824 | bytes 1180674 | tf_op jit(solution)/shard_map/scatter | solution.py:48
  15.3 7.3 %all-to-all-start.1 = ((bf16[8,64,768]{2,1,0:T(8,128)(2,1)}), bf16[8,64,768]{2,1,0:T(8,128)(2,1)S(1)}, u32[]{:S(2)}, u32[]{:S(2)}) async-start(bf16[8,64,768]{2,1,0:T(8,128)(2,1)} %bitcast.7), calls=%async_computation.1 | async-start | bytes 1572864 | tf_op jit(solution)/shard_map/all_to_all | solution.py:51
  24.1 1.4 scatter_custom_fusion
  26.7 16.9 %all-to-all-done.1 = bf16[8,64,768]{2,1,0:T(8,128)(2,1)S(1)} async-done(((bf16[8,64,768]{2,1,0:T(8,128)(2,1)}), bf16[8,64,768]{2,1,0:T(8,128)(2,1)S(1)}, u32[]{:S(2)}, u32[]{:S(2)}) %all-to-all-start.1) | async-done | bytes 786464 | tf_op jit(solution)/shard_map/all_to_all | solution.py:51
  43.6 3.5 %all-to-all-start = ((s32[8,1,64]{2,1,0:T(1,128)}), s32[8,1,64]{2,1,0:T(1,128)S(1)}, u32[]{:S(2)}, u32[]{:S(2)}) async-start(s32[8,1,64]{2,1,0:T(1,128)} %all_to_all.13), calls=%async_computation | async-start | bytes 8192 | tf_op jit(solution)/shard_map/all_to_all | solution.py:58
  48.3 5.2 %all-to-all-done = s32[8,1,64]{2,1,0:T(1,128)S(1)} async-done(((s32[8,1,64]{2,1,0:T(1,128)}), s32[8,1,64]{2,1,0:T(1,128)S(1)}, u32[]{:S(2)}, u32[]{:S(2)}) %all-to-all-start) | async-done | bytes 2080 | tf_op jit(solution)/shard_map/all_to_all | solution.py:58
  53.7 1.8 all-gather
  56.1 4.3 %scatter_custom_fusion.2 = s32[256]{0:T(256)S(1)} fusion(s32[1024]{0:T(1024)S(1)} %compare_select_fusion, s32[1024]{0:T(1024)S(1)} %bitcast.49, s32[]{:T(128)} %constant.19.clone.1), kind=kCustom, calls=%fused_computation.53 | custom fusion | bytes 1028 | tf_op jit(solution)/shard_map/scatter | solution.py:82
  60.4 1.3 collective-permute-start.2
  61.7 5.1 %collective-permute-start = (s32[256]{0:T(256)S(1)}, s32[256]{0:T(256)}, u32[]{:S(2)}, u32[]{:S(2)}) collective-permute-start(s32[256]{0:T(256)S(1)} %scatter_custom_fusion.2), channel_id=1, source_target_pairs={{0,2},{2,4},{4,6},{6,8},{8,10},{10,12},{12,14},{1,3},{3,5},{5,7},{... | collective-permute-start | bytes 3080 | tf_op jit(solution)/shard_map/ppermute | solution.py:12
  68.6 1.3 collective-permute-start.6
  69.9 5.1 %collective-permute-start.4 = (s32[256]{0:T(256)}, s32[256]{0:T(256)}, u32[]{:S(2)}, u32[]{:S(2)}) collective-permute-start(s32[256]{0:T(256)} %collective-permute-done), channel_id=1, source_target_pairs={{0,2},{2,4},{4,6},{6,8},{8,10},{10,12},{12,14},{1,3},{3,5},{5,7},{... | collective-permute-start | bytes 3080 | tf_op jit(solution)/shard_map/ppermute | solution.py:12
  75.0 47.2 %all-reduce.2.cloned.1.call-done = f32[128,768]{1,0:T(8,128)} async-done(((f32[128,768]{1,0:T(8,128)}), f32[128,768]{1,0:T(8,128)}) %all-reduce.2.cloned.1.call-update) | async-done | bytes 393232 | tf_op jit(solution)/shard_map/psum | solution.py:99
  123.4 5.7 %scatter_custom_fusion.3 = bf16[256,768]{1,0:T(8,128)(2,1)S(1)} fusion(s32[1024]{0:T(1024)S(1)} %compare_select_fusion, bf16[1024,768]{1,0:T(8,128)(2,1)} %all-gather.3.cloned.1.call-done, bf16[]{:T(256)} %constant.23.clone.1), kind=kCustom, calls=%fused_computation.21 | custom fusion | bytes 393728 | tf_op jit(solution)/shard_map/scatter | solution.py:81
  129.1 1.3 collective-permute-start.3
  130.4 4.6 %collective-permute-start.1 = (bf16[256,768]{1,0:T(8,128)(2,1)S(1)}, bf16[256,768]{1,0:T(8,128)(2,1)S(1)}, u32[]{:S(2)}, u32[]{:S(2)}) collective-permute-start(bf16[256,768]{1,0:T(8,128)(2,1)S(1)} %scatter_custom_fusion.3), channel_id=1, source_target_pairs={{0,2},{2,4},{4,6},{6,8},{8,10},{10,12},{12,14},{1,3},{3,5},{5,7},{... | collective-permute-start | bytes 1179656 | tf_op jit(solution)/shard_map/ppermute | solution.py:12
  136.1 1.4 gather_fusion.1
  137.5 2.8 %select_reduce_fusion = f32[512]{0:T(512)S(1)} fusion(bf16[512,768]{1,0:T(8,128)(2,1)S(1)} %bitcast.41, bf16[1024,768]{1,0:T(8,128)(2,1)} %all-gather.3.cloned.1.call-done, s32[1024]{0:T(1024)S(1)} %bitcast.50, s32[512]{0:T(512)} %iota_add_fusion, s32[512]{0:T(512)S(1)} %eq.145, pred[512]{0:T(512)(128)(4,1)} %broadcast_compare_fusion.1), kind=kOutput, calls=%fused_computation.6 | convolution fusion | flops 808451584 | bytes 2370048 | tf_op jit(solution)/shard_map/dot_general | solution.py:22
  142.3 6.2 %collective-permute-done.1 = bf16[256,768]{1,0:T(8,128)(2,1)S(1)} collective-permute-done((bf16[256,768]{1,0:T(8,128)(2,1)S(1)}, bf16[256,768]{1,0:T(8,128)(2,1)S(1)}, u32[]{:S(2)}, u32[]{:S(2)}) %collective-permute-start.1) | collective-permute-done | bytes 393248 | tf_op jit(solution)/shard_map/ppermute | solution.py:12
  148.5 4.4 %collective-permute-start.5 = (bf16[256,768]{1,0:T(8,128)(2,1)S(1)}, bf16[256,768]{1,0:T(8,128)(2,1)S(1)}, u32[]{:S(2)}, u32[]{:S(2)}) collective-permute-start(bf16[256,768]{1,0:T(8,128)(2,1)S(1)} %collective-permute-done.1), channel_id=1, source_target_pairs={{0,2},{2,4},{4,6},{6,8},{8,10},{10,12},{12,14},{1,3},{3,5},{5,7},{... | collective-permute-start | bytes 1179656 | tf_op jit(solution)/shard_map/ppermute | solution.py:12
  154.1 11.3 %collective-permute-done.5 = bf16[256,768]{1,0:T(8,128)(2,1)S(1)} collective-permute-done((bf16[256,768]{1,0:T(8,128)(2,1)S(1)}, bf16[256,768]{1,0:T(8,128)(2,1)S(1)}, u32[]{:S(2)}, u32[]{:S(2)}) %collective-permute-start.5) | collective-permute-done | bytes 393248 | tf_op jit(solution)/shard_map/ppermute | solution.py:12
  167.4 5.9 %all-to-all-start.2 = ((f32[8,1,64]{2,1,0:T(1,128)}), f32[8,1,64]{2,1,0:T(1,128)S(1)}, u32[]{:S(2)}, u32[]{:S(2)}) async-start(f32[8,1,64]{2,1,0:T(1,128)} %max.65), calls=%async_computation.2 | async-start | bytes 8192 | tf_op jit(solution)/shard_map/all_to_all | solution.py:103
  174.1 5.7 %all-to-all-done.2 = f32[8,1,64]{2,1,0:T(1,128)S(1)} async-done(((f32[8,1,64]{2,1,0:T(1,128)}), f32[8,1,64]{2,1,0:T(1,128)S(1)}, u32[]{:S(2)}, u32[]{:S(2)}) %all-to-all-start.2) | async-done | bytes 2080 | tf_op jit(solution)/shard_map/all_to_all | solution.py:103
  181.1 2.5 %gather_fusion = f32[256]{0:T(256)} fusion(f32[512]{0:T(512)S(1)} %reshape.165, s32[1024]{0:T(1024)S(1)} %pad_clamp_fusion.1), kind=kCustom, calls=%fused_computation | custom fusion | bytes 3072 | tf_op jit(solution)/shard_map/gather | solution.py:106
  (69 shorter events, 19.9 us)
Async XLA Ops:
  8.0 14.9 %copy-start.2 = (bf16[256,768]{1,0:T(8,128)(2,1)S(1)}, bf16[256,768]{1,0:T(8,128)(2,1)}, u32[]{:S(2)}) copy-start(bf16[256,768]{1,0:T(8,128)(2,1)} %param.4) | copy-start | bytes 1179652
  8.0 14.7 %copy-start.3 = (s32[256,1]{0,1:T(1,128)S(1)}, s32[256,1]{0,1:T(1,128)}, u32[]{:S(2)}) copy-start(s32[256,1]{0,1:T(1,128)} %param.5) | copy-start | bytes 3076
  8.0 14.7 %copy-start.4 = (s32[256]{0:T(256)S(1)}, s32[256]{0:T(256)}, u32[]{:S(2)}) copy-start(s32[256]{0:T(256)} %param.6) | copy-start | bytes 3076
  8.0 14.7 %copy-start.5 = (s32[128]{0:T(128)S(1)}, s32[128]{0:T(128)}, u32[]{:S(2)}) copy-start(s32[128]{0:T(128)} %param.7) | copy-start | bytes 1540
  15.3 28.3 %all-to-all-start.1 = ((bf16[8,64,768]{2,1,0:T(8,128)(2,1)}), bf16[8,64,768]{2,1,0:T(8,128)(2,1)S(1)}, u32[]{:S(2)}, u32[]{:S(2)}) async-start(bf16[8,64,768]{2,1,0:T(8,128)(2,1)} %bitcast.7), calls=%async_computation.1 | async-start | bytes 1572864 | tf_op jit(solution)/shard_map/all_to_all | solution.py:51
  22.6 99.6 %all-reduce.2.cloned.1.call-start = ((), (), s32[]{:S(2)}) async-start(), calls=%async_computation.4 | async-start | bytes 786432 | tf_op jit(solution)/shard_map/psum | solution.py:99
  43.6 3.5 %copy-start = (bf16[8,64,768]{2,1,0:T(8,128)(2,1)}, bf16[8,64,768]{2,1,0:T(8,128)(2,1)S(1)}, u32[]{:S(2)}) copy-start(bf16[8,64,768]{2,1,0:T(8,128)(2,1)S(1)} %all-to-all-done.1) | copy-start | bytes 2359300
  43.6 10.0 %all-to-all-start = ((s32[8,1,64]{2,1,0:T(1,128)}), s32[8,1,64]{2,1,0:T(1,128)S(1)}, u32[]{:S(2)}, u32[]{:S(2)}) async-start(s32[8,1,64]{2,1,0:T(1,128)} %all_to_all.13), calls=%async_computation | async-start | bytes 8192 | tf_op jit(solution)/shard_map/all_to_all | solution.py:58
  47.1 76.3 %all-gather.3.cloned.1.call-start = ((), (), s32[]{:S(2)}) async-start(), calls=%async_computation.3 | async-start | bytes 2359296 | tf_op jit(solution)/shard_map/all_gather | solution.py:65
  60.4 8.2 %collective-permute-start.2 = (s32[256]{0:T(256)S(1)}, s32[256]{0:T(256)}, u32[]{:S(2)}, u32[]{:S(2)}) collective-permute-start(s32[256]{0:T(256)S(1)} %scatter_custom_fusion.2), channel_id=1, source_target_pairs={{2,0},{4,2},{6,4},{8,6},{10,8},{12,10},{14,12},{3,1},{5,3},{7,5},{... | collective-permute-start | bytes 3080 | tf_op jit(solution)/shard_map/ppermute | solution.py:12
  61.7 8.2 %collective-permute-start = (s32[256]{0:T(256)S(1)}, s32[256]{0:T(256)}, u32[]{:S(2)}, u32[]{:S(2)}) collective-permute-start(s32[256]{0:T(256)S(1)} %scatter_custom_fusion.2), channel_id=1, source_target_pairs={{0,2},{2,4},{4,6},{6,8},{8,10},{10,12},{12,14},{1,3},{3,5},{5,7},{... | collective-permute-start | bytes 3080 | tf_op jit(solution)/shard_map/ppermute | solution.py:12
  68.6 85.5 %collective-permute-start.6 = (s32[256]{0:T(256)}, s32[256]{0:T(256)}, u32[]{:S(2)}, u32[]{:S(2)}) collective-permute-start(s32[256]{0:T(256)} %collective-permute-done.2), channel_id=1, source_target_pairs={{2,0},{4,2},{6,4},{8,6},{10,8},{12,10},{14,12},{3,1},{5,3},{7,5},{... | collective-permute-start | bytes 3080 | tf_op jit(solution)/shard_map/ppermute | solution.py:12
  69.9 84.3 %collective-permute-start.4 = (s32[256]{0:T(256)}, s32[256]{0:T(256)}, u32[]{:S(2)}, u32[]{:S(2)}) collective-permute-start(s32[256]{0:T(256)} %collective-permute-done), channel_id=1, source_target_pairs={{0,2},{2,4},{4,6},{6,8},{8,10},{10,12},{12,14},{1,3},{3,5},{5,7},{... | collective-permute-start | bytes 3080 | tf_op jit(solution)/shard_map/ppermute | solution.py:12
  129.1 11.9 %collective-permute-start.3 = (bf16[256,768]{1,0:T(8,128)(2,1)S(1)}, bf16[256,768]{1,0:T(8,128)(2,1)S(1)}, u32[]{:S(2)}, u32[]{:S(2)}) collective-permute-start(bf16[256,768]{1,0:T(8,128)(2,1)S(1)} %scatter_custom_fusion.3), channel_id=1, source_target_pairs={{2,0},{4,2},{6,4},{8,6},{10,8},{12,10},{14,12},{3,1},{5,3},{7,5},{... | collective-permute-start | bytes 1179656 | tf_op jit(solution)/shard_map/ppermute | solution.py:12
  130.4 18.0 %collective-permute-start.1 = (bf16[256,768]{1,0:T(8,128)(2,1)S(1)}, bf16[256,768]{1,0:T(8,128)(2,1)S(1)}, u32[]{:S(2)}, u32[]{:S(2)}) collective-permute-start(bf16[256,768]{1,0:T(8,128)(2,1)S(1)} %scatter_custom_fusion.3), channel_id=1, source_target_pairs={{0,2},{2,4},{4,6},{6,8},{8,10},{10,12},{12,14},{1,3},{3,5},{5,7},{... | collective-permute-start | bytes 1179656 | tf_op jit(solution)/shard_map/ppermute | solution.py:12
  136.1 1.4 copy-start.1
  141.0 12.7 %collective-permute-start.7 = (bf16[256,768]{1,0:T(8,128)(2,1)S(1)}, bf16[256,768]{1,0:T(8,128)(2,1)S(1)}, u32[]{:S(2)}, u32[]{:S(2)}) collective-permute-start(bf16[256,768]{1,0:T(8,128)(2,1)S(1)} %collective-permute-done.3), channel_id=1, source_target_pairs={{2,0},{4,2},{6,4},{8,6},{10,8},{12,10},{14,12},{3,1},{5,3},{7,5},{... | collective-permute-start | bytes 1179656 | tf_op jit(solution)/shard_map/ppermute | solution.py:12
  148.5 17.0 %collective-permute-start.5 = (bf16[256,768]{1,0:T(8,128)(2,1)S(1)}, bf16[256,768]{1,0:T(8,128)(2,1)S(1)}, u32[]{:S(2)}, u32[]{:S(2)}) collective-permute-start(bf16[256,768]{1,0:T(8,128)(2,1)S(1)} %collective-permute-done.1), channel_id=1, source_target_pairs={{0,2},{2,4},{4,6},{6,8},{8,10},{10,12},{12,14},{1,3},{3,5},{5,7},{... | collective-permute-start | bytes 1179656 | tf_op jit(solution)/shard_map/ppermute | solution.py:12
  153.3 12.2 %copy-start.6 = (pred[512]{0:T(512)(128)(4,1)S(1)}, pred[512]{0:T(512)(128)(4,1)}, u32[]{:S(2)}) copy-start(pred[512]{0:T(512)(128)(4,1)} %broadcast_compare_fusion.1) | copy-start | bytes 1540
  167.4 12.4 %all-to-all-start.2 = ((f32[8,1,64]{2,1,0:T(1,128)}), f32[8,1,64]{2,1,0:T(1,128)S(1)}, u32[]{:S(2)}, u32[]{:S(2)}) async-start(f32[8,1,64]{2,1,0:T(1,128)} %max.65), calls=%async_computation.2 | async-start | bytes 8192 | tf_op jit(solution)/shard_map/all_to_all | solution.py:103
Sparse Core Ops, SparseCore 0:
  26.8 95.4 all-reduce.1
Sparse Core Ops, SparseCore 1:
  49.1 11.1 all-gather.2
where the time goes:
time: 192 us; the launch traced here: 191 us
  waiting for transfers between devices  93.8 us (49%)
  starting transfers between devices  41.1 us (21%)
  local copies, waits for them, and re-layouts  18.3 us (10%)
  between operations  15.8 us (8%)
  other arithmetic  13.8 us (7%)
  matrix products  6.34 us (3%)
    psum x1, waiting for transfers between devices, body(): sums = lax.psum(partial_sums, ('blk', 'span'))  47.2 us
    ppermute x8, starting transfers between devices, passed_along(): lax.ppermute(value, axis, [(source, source + steps) for source in range(f...  24.3 us
    ppermute x8, waiting for transfers between devices, passed_along(): lax.ppermute(value, axis, [(source, source + steps) for source in range(f...  18.2 us
    all_to_all x1, waiting for transfers between devices, body(): lax.all_to_all(send_rows.reshape(owners, capacity, width), 'blk', split_a...  16.9 us
    all_to_all x1, starting transfers between devices, body(): lax.all_to_all(send_rows.reshape(owners, capacity, width), 'blk', split_a...  7.31 us
    all_to_all x1, starting transfers between devices, body(): lax.all_to_all(best.reshape(owners, capacity), 'blk', split_axis=0, conca...  5.92 us
    scatter x1, local copies, waits for them, and re-layouts, body(): jnp.zeros((share_limit, width), jnp.bfloat16).at[target]  5.74 us
    all_to_all x1, waiting for transfers between devices, body(): lax.all_to_all(best.reshape(owners, capacity), 'blk', split_axis=0, conca...  5.68 us
  transfers between devices with their start and end apart: 13, of which 7 were waited for; matrix products, arithmetic and copies ran while one was open for 13% of the time, Pallas kernels for 0%

commit v1 on v0

--- a/solution.py
+++ b/solution.py
@@ -4,6 +4,14 @@
 from jax.sharding import PartitionSpec as P
 
 GIANT_SPAN = 3
+
+
+def slots_view(shard_in):
+    device_axis = "blk"
+    chip_axis = "span"
+    for it in (chip_axis, device_axis):
+        shard_in = lax.psum(shard_in, axis_name=it)
+    return shard_in
 
 
 def passed_along(value, axis, steps):
@@ -96,7 +104,7 @@
         (((0,), (0,)), ((), ())),
         preferred_element_type=jnp.float32,
     )
-    sums = lax.psum(partial_sums, ("blk", "span"))
+    sums = slots_view(partial_sums)
     length = jnp.sqrt(jnp.sum(sums * sums, axis=1, keepdims=True))
     direction = sums / jnp.maximum(length, 1.0)
     centroid_cosine = jnp.sum(unit.astype(jnp.float32) * direction[cluster], axis=1)

time: 192 us -> 205 us (1.068)
  waiting for transfers between devices: 93.8 us -> 106 us
  starting transfers between devices: 41.1 us -> 43.9 us
    all_to_all x1, waiting for transfers between devices: 16.9 us -> 0.01 us  [body(): lax.all_to_all(send_rows.reshape(owners, capacity, width), 'blk', split_a...]
    psum x1 -> x2, waiting for transfers between devices: 47.2 us -> 61.4 us  [slots_view(): shard_in = lax.psum(shard_in, axis_name=it)]
    all_gather x1, waiting for transfers between devices: 0.03 us -> 9.31 us  [body(): lax.all_gather(mine, 'span', axis=0, tiled=True)]
    ppermute x8, waiting for transfers between devices: 18.2 us -> 23.3 us  [passed_along(): lax.ppermute(value, axis, [(source, source + steps) for source in range(f...]
    all_to_all x1, starting transfers between devices: 3.48 us -> 5.83 us  [body(): lax.all_to_all(send_tags.reshape(owners, capacity), 'blk', split_axis=0,...]
  transfers between devices with their start and end apart: 13 -> 14, of which waited for: 7 -> 8; matrix products, arithmetic and copies ran while one was open for 13% -> 12% of each run, Pallas kernels for 0% -> 0%
where the time goes in v1:
time: 205 us; the launch traced here: 204 us
  waiting for transfers between devices  106 us (52%)
  starting transfers between devices  43.9 us (21%)
  local copies, waits for them, and re-layouts  18.3 us (9%)
  between operations  14.1 us (7%)
  other arithmetic  13.8 us (7%)
  matrix products  6.31 us (3%)
    psum x2, waiting for transfers between devices, slots_view(): shard_in = lax.psum(shard_in, axis_name=it)  61.4 us
    ppermute x8, starting transfers between devices, passed_along(): lax.ppermute(value, axis, [(source, source + steps) for source in range(f...  24.3 us
    ppermute x8, waiting for transfers between devices, passed_along(): lax.ppermute(value, axis, [(source, source + steps) for source in range(f...  23.3 us
    all_gather x1, waiting for transfers between devices, body(): lax.all_gather(mine, 'span', axis=0, tiled=True)  9.31 us
    all_to_all x1, starting transfers between devices, body(): lax.all_to_all(send_rows.reshape(owners, capacity, width), 'blk', split_a...  7.31 us
    all_to_all x1, starting transfers between devices, body(): lax.all_to_all(best.reshape(owners, capacity), 'blk', split_axis=0, conca...  6.32 us
    all_to_all x1, starting transfers between devices, body(): lax.all_to_all(send_tags.reshape(owners, capacity), 'blk', split_axis=0,...  5.83 us
    scatter x1, local copies, waits for them, and re-layouts, body(): jnp.zeros((share_limit, width), jnp.bfloat16).at[target]  5.73 us
  transfers between devices with their start and end apart: 14, of which 8 were waited for; matrix products, arithmetic and copies ran while one was open for 12% of the time, Pallas kernels for 0%

profile of v1, /device:TPU:0, one launch (start us, length us, event | category | flops | bytes accessed | tf_op | source)
XLA Modules:
  0.0 203.8 jit_solution(13111134576609811754)
XLA Ops:
  11.4 3.1 %scatter_custom_fusion.1 = bf16[512,768]{1,0:T(8,128)(2,1)} fusion(s32[256]{0:T(256)S(1)} %bitcast.54, bf16[]{:T(256)} %constant.23.clone.1, bf16[256,768]{1,0:T(8,128)(2,1)} %param.4, f32[256]{0:T(256)S(1)} %add_rsqrt_fusion), kind=kCustom, calls=%fused_computation.18 | custom fusion | flops 589824 | bytes 1180674 | tf_op jit(solution)/shard_map/scatter | solution.py:56
  14.5 7.3 %all-to-all-start.1 = ((bf16[8,64,768]{2,1,0:T(8,128)(2,1)}), bf16[8,64,768]{2,1,0:T(8,128)(2,1)S(1)}, u32[]{:S(2)}, u32[]{:S(2)}) async-start(bf16[8,64,768]{2,1,0:T(8,128)(2,1)} %bitcast.7), calls=%async_computation.1 | async-start | bytes 1572864 | tf_op jit(solution)/shard_map/all_to_all | solution.py:59
  23.2 21.5 %all-reduce.3.cloned.1.call-done = f32[128,768]{1,0:T(8,128)} async-done(((f32[128,768]{1,0:T(8,128)}), f32[128,768]{1,0:T(8,128)}) %all-reduce.3.cloned.1.call-update) | async-done | bytes 393232 | tf_op jit(solution)/shard_map/psum | solution.py:13
  44.8 1.4 scatter_custom_fusion
  47.5 5.8 %all-to-all-start = ((s32[8,1,64]{2,1,0:T(1,128)}), s32[8,1,64]{2,1,0:T(1,128)S(1)}, u32[]{:S(2)}, u32[]{:S(2)}) async-start(s32[8,1,64]{2,1,0:T(1,128)} %all_to_all.13), calls=%async_computation | async-start | bytes 8192 | tf_op jit(solution)/shard_map/all_to_all | solution.py:66
  54.8 5.1 %all-to-all-done = s32[8,1,64]{2,1,0:T(1,128)S(1)} async-done(((s32[8,1,64]{2,1,0:T(1,128)}), s32[8,1,64]{2,1,0:T(1,128)S(1)}, u32[]{:S(2)}, u32[]{:S(2)}) %all-to-all-start) | async-done | bytes 2080 | tf_op jit(solution)/shard_map/all_to_all | solution.py:66
  59.9 1.8 all-gather
  62.4 4.3 %scatter_custom_fusion.2 = s32[256]{0:T(256)S(1)} fusion(s32[1024]{0:T(1024)S(1)} %compare_select_fusion, s32[1024]{0:T(1024)S(1)} %bitcast.49, s32[]{:T(128)} %constant.19.clone.1), kind=kCustom, calls=%fused_computation.53 | custom fusion | bytes 1028 | tf_op jit(solution)/shard_map/scatter | solution.py:90
  68.0 5.1 %collective-permute-start = (s32[256]{0:T(256)S(1)}, s32[256]{0:T(256)}, u32[]{:S(2)}, u32[]{:S(2)}) collective-permute-start(s32[256]{0:T(256)S(1)} %scatter_custom_fusion.2), channel_id=1, source_target_pairs={{0,2},{2,4},{4,6},{6,8},{8,10},{10,12},{12,14},{1,3},{3,5},{5,7},{... | collective-permute-start | bytes 3080 | tf_op jit(solution)/shard_map/ppermute | solution.py:20
  76.1 5.1 %collective-permute-start.4 = (s32[256]{0:T(256)}, s32[256]{0:T(256)}, u32[]{:S(2)}, u32[]{:S(2)}) collective-permute-start(s32[256]{0:T(256)} %collective-permute-done), channel_id=1, source_target_pairs={{0,2},{2,4},{4,6},{6,8},{8,10},{10,12},{12,14},{1,3},{3,5},{5,7},{... | collective-permute-start | bytes 3080 | tf_op jit(solution)/shard_map/ppermute | solution.py:20
  81.3 39.9 %all-reduce.5.cloned.1.call-done = f32[128,768]{1,0:T(8,128)} async-done(((f32[128,768]{1,0:T(8,128)}), f32[128,768]{1,0:T(8,128)}) %all-reduce.5.cloned.1.call-update) | async-done | bytes 393232 | tf_op jit(solution)/shard_map/psum | solution.py:13
  122.3 9.3 %all-gather.3.cloned.1.call-done = bf16[1024,768]{1,0:T(8,128)(2,1)} async-done(((bf16[512,768]{1,0:T(8,128)(2,1)}), bf16[1024,768]{1,0:T(8,128)(2,1)}) %all-gather.3.cloned.1.call-update) | async-done | bytes 1572880 | tf_op jit(solution)/shard_map/all_gather | solution.py:73
  131.6 5.7 %scatter_custom_fusion.3 = bf16[256,768]{1,0:T(8,128)(2,1)S(1)} fusion(s32[1024]{0:T(1024)S(1)} %compare_select_fusion, bf16[1024,768]{1,0:T(8,128)(2,1)} %all-gather.3.cloned.1.call-done, bf16[]{:T(256)} %constant.23.clone.1), kind=kCustom, calls=%fused_computation.21 | custom fusion | bytes 393728 | tf_op jit(solution)/shard_map/scatter | solution.py:89
  137.3 1.3 collective-permute-start.3
  138.6 4.6 %collective-permute-start.1 = (bf16[256,768]{1,0:T(8,128)(2,1)S(1)}, bf16[256,768]{1,0:T(8,128)(2,1)S(1)}, u32[]{:S(2)}, u32[]{:S(2)}) collective-permute-start(bf16[256,768]{1,0:T(8,128)(2,1)S(1)} %scatter_custom_fusion.3), channel_id=1, source_target_pairs={{0,2},{2,4},{4,6},{6,8},{8,10},{10,12},{12,14},{1,3},{3,5},{5,7},{... | collective-permute-start | bytes 1179656 | tf_op jit(solution)/shard_map/ppermute | solution.py:20
  144.3 1.4 gather_fusion.1
  145.7 2.8 %select_reduce_fusion = f32[512]{0:T(512)S(1)} fusion(bf16[512,768]{1,0:T(8,128)(2,1)S(1)} %bitcast.41, bf16[1024,768]{1,0:T(8,128)(2,1)} %all-gather.3.cloned.1.call-done, s32[1024]{0:T(1024)S(1)} %bitcast.50, s32[512]{0:T(512)} %iota_add_fusion, s32[512]{0:T(512)S(1)} %eq.145, pred[512]{0:T(512)(128)(4,1)} %broadcast_compare_fusion.1), kind=kOutput, calls=%fused_computation.6 | convolution fusion | flops 808451584 | bytes 2370048 | tf_op jit(solution)/shard_map/dot_general | solution.py:30
  148.5 2.1 %collective-permute-done.3 = bf16[256,768]{1,0:T(8,128)(2,1)S(1)} collective-permute-done((bf16[256,768]{1,0:T(8,128)(2,1)S(1)}, bf16[256,768]{1,0:T(8,128)(2,1)S(1)}, u32[]{:S(2)}, u32[]{:S(2)}) %collective-permute-start.3) | collective-permute-done | bytes 393248 | tf_op jit(solution)/shard_map/ppermute | solution.py:20
  151.8 7.3 %collective-permute-done.1 = bf16[256,768]{1,0:T(8,128)(2,1)S(1)} collective-permute-done((bf16[256,768]{1,0:T(8,128)(2,1)S(1)}, bf16[256,768]{1,0:T(8,128)(2,1)S(1)}, u32[]{:S(2)}, u32[]{:S(2)}) %collective-permute-start.1) | collective-permute-done | bytes 393248 | tf_op jit(solution)/shard_map/ppermute | solution.py:20
  159.1 4.4 %collective-permute-start.5 = (bf16[256,768]{1,0:T(8,128)(2,1)S(1)}, bf16[256,768]{1,0:T(8,128)(2,1)S(1)}, u32[]{:S(2)}, u32[]{:S(2)}) collective-permute-start(bf16[256,768]{1,0:T(8,128)(2,1)S(1)} %collective-permute-done.1), channel_id=1, source_target_pairs={{0,2},{2,4},{4,6},{6,8},{8,10},{10,12},{12,14},{1,3},{3,5},{5,7},{... | collective-permute-start | bytes 1179656 | tf_op jit(solution)/shard_map/ppermute | solution.py:20
  164.8 13.9 %collective-permute-done.5 = bf16[256,768]{1,0:T(8,128)(2,1)S(1)} collective-permute-done((bf16[256,768]{1,0:T(8,128)(2,1)S(1)}, bf16[256,768]{1,0:T(8,128)(2,1)S(1)}, u32[]{:S(2)}, u32[]{:S(2)}) %collective-permute-start.5) | collective-permute-done | bytes 393248 | tf_op jit(solution)/shard_map/ppermute | solution.py:20
  180.7 6.3 %all-to-all-start.2 = ((f32[8,1,64]{2,1,0:T(1,128)}), f32[8,1,64]{2,1,0:T(1,128)S(1)}, u32[]{:S(2)}, u32[]{:S(2)}) async-start(f32[8,1,64]{2,1,0:T(1,128)} %max.65), calls=%async_computation.2 | async-start | bytes 8192 | tf_op jit(solution)/shard_map/all_to_all | solution.py:111
  187.8 5.7 %all-to-all-done.2 = f32[8,1,64]{2,1,0:T(1,128)S(1)} async-done(((f32[8,1,64]{2,1,0:T(1,128)}), f32[8,1,64]{2,1,0:T(1,128)S(1)}, u32[]{:S(2)}, u32[]{:S(2)}) %all-to-all-start.2) | async-done | bytes 2080 | tf_op jit(solution)/shard_map/all_to_all | solution.py:111
  194.8 2.5 %gather_fusion = f32[256]{0:T(256)} fusion(f32[512]{0:T(512)S(1)} %reshape.165, s32[1024]{0:T(1024)S(1)} %pad_clamp_fusion.1), kind=kCustom, calls=%fused_computation | custom fusion | bytes 3072 | tf_op jit(solution)/shard_map/gather | solution.py:114
  (72 shorter events, 21.9 us)
Async XLA Ops:
  7.2 14.9 %copy-start.2 = (bf16[256,768]{1,0:T(8,128)(2,1)S(1)}, bf16[256,768]{1,0:T(8,128)(2,1)}, u32[]{:S(2)}) copy-start(bf16[256,768]{1,0:T(8,128)(2,1)} %param.4) | copy-start | bytes 1179652
  7.2 14.7 %copy-start.3 = (s32[256,1]{0,1:T(1,128)S(1)}, s32[256,1]{0,1:T(1,128)}, u32[]{:S(2)}) copy-start(s32[256,1]{0,1:T(1,128)} %param.5) | copy-start | bytes 3076
  7.2 14.7 %copy-start.4 = (s32[256]{0:T(256)S(1)}, s32[256]{0:T(256)}, u32[]{:S(2)}) copy-start(s32[256]{0:T(256)} %param.6) | copy-start | bytes 3076
  7.2 14.7 %copy-start.5 = (s32[128]{0:T(128)S(1)}, s32[128]{0:T(128)}, u32[]{:S(2)}) copy-start(s32[128]{0:T(128)} %param.7) | copy-start | bytes 1540
  14.5 33.0 %all-to-all-start.1 = ((bf16[8,64,768]{2,1,0:T(8,128)(2,1)}), bf16[8,64,768]{2,1,0:T(8,128)(2,1)S(1)}, u32[]{:S(2)}, u32[]{:S(2)}) async-start(bf16[8,64,768]{2,1,0:T(8,128)(2,1)} %bitcast.7), calls=%async_computation.1 | async-start | bytes 1572864 | tf_op jit(solution)/shard_map/all_to_all | solution.py:59
  21.8 23.0 %all-reduce.3.cloned.1.call-start = ((), (), s32[]{:S(2)}) async-start(), calls=%async_computation.4 | async-start | bytes 786432 | tf_op jit(solution)/shard_map/psum | solution.py:13
  23.2 98.0 %all-reduce.5.cloned.1.call-start = ((), (), s32[]{:S(2)}) async-start(), calls=%async_computation.5 | async-start | bytes 786432 | tf_op jit(solution)/shard_map/psum | solution.py:13
  47.5 5.9 %copy-start = (bf16[8,64,768]{2,1,0:T(8,128)(2,1)}, bf16[8,64,768]{2,1,0:T(8,128)(2,1)S(1)}, u32[]{:S(2)}) copy-start(bf16[8,64,768]{2,1,0:T(8,128)(2,1)S(1)} %all-to-all-done.1) | copy-start | bytes 2359300
  47.5 12.3 %all-to-all-start = ((s32[8,1,64]{2,1,0:T(1,128)}), s32[8,1,64]{2,1,0:T(1,128)S(1)}, u32[]{:S(2)}, u32[]{:S(2)}) async-start(s32[8,1,64]{2,1,0:T(1,128)} %all_to_all.13), calls=%async_computation | async-start | bytes 8192 | tf_op jit(solution)/shard_map/all_to_all | solution.py:66
  53.3 78.3 %all-gather.3.cloned.1.call-start = ((), (), s32[]{:S(2)}) async-start(), calls=%async_computation.3 | async-start | bytes 2359296 | tf_op jit(solution)/shard_map/all_gather | solution.py:73
  66.7 8.2 %collective-permute-start.2 = (s32[256]{0:T(256)S(1)}, s32[256]{0:T(256)}, u32[]{:S(2)}, u32[]{:S(2)}) collective-permute-start(s32[256]{0:T(256)S(1)} %scatter_custom_fusion.2), channel_id=1, source_target_pairs={{2,0},{4,2},{6,4},{8,6},{10,8},{12,10},{14,12},{3,1},{5,3},{7,5},{... | collective-permute-start | bytes 3080 | tf_op jit(solution)/shard_map/ppermute | solution.py:20
  68.0 8.2 %collective-permute-start = (s32[256]{0:T(256)S(1)}, s32[256]{0:T(256)}, u32[]{:S(2)}, u32[]{:S(2)}) collective-permute-start(s32[256]{0:T(256)S(1)} %scatter_custom_fusion.2), channel_id=1, source_target_pairs={{0,2},{2,4},{4,6},{6,8},{8,10},{10,12},{12,14},{1,3},{3,5},{5,7},{... | collective-permute-start | bytes 3080 | tf_op jit(solution)/shard_map/ppermute | solution.py:20
  74.8 89.9 %collective-permute-start.6 = (s32[256]{0:T(256)}, s32[256]{0:T(256)}, u32[]{:S(2)}, u32[]{:S(2)}) collective-permute-start(s32[256]{0:T(256)} %collective-permute-done.2), channel_id=1, source_target_pairs={{2,0},{4,2},{6,4},{8,6},{10,8},{12,10},{14,12},{3,1},{5,3},{7,5},{... | collective-permute-start | bytes 3080 | tf_op jit(solution)/shard_map/ppermute | solution.py:20
  76.1 88.6 %collective-permute-start.4 = (s32[256]{0:T(256)}, s32[256]{0:T(256)}, u32[]{:S(2)}, u32[]{:S(2)}) collective-permute-start(s32[256]{0:T(256)} %collective-permute-done), channel_id=1, source_target_pairs={{0,2},{2,4},{4,6},{6,8},{8,10},{10,12},{12,14},{1,3},{3,5},{5,7},{... | collective-permute-start | bytes 3080 | tf_op jit(solution)/shard_map/ppermute | solution.py:20
  137.3 13.2 %collective-permute-start.3 = (bf16[256,768]{1,0:T(8,128)(2,1)S(1)}, bf16[256,768]{1,0:T(8,128)(2,1)S(1)}, u32[]{:S(2)}, u32[]{:S(2)}) collective-permute-start(bf16[256,768]{1,0:T(8,128)(2,1)S(1)} %scatter_custom_fusion.3), channel_id=1, source_target_pairs={{2,0},{4,2},{6,4},{8,6},{10,8},{12,10},{14,12},{3,1},{5,3},{7,5},{... | collective-permute-start | bytes 1179656 | tf_op jit(solution)/shard_map/ppermute | solution.py:20
  138.6 20.5 %collective-permute-start.1 = (bf16[256,768]{1,0:T(8,128)(2,1)S(1)}, bf16[256,768]{1,0:T(8,128)(2,1)S(1)}, u32[]{:S(2)}, u32[]{:S(2)}) collective-permute-start(bf16[256,768]{1,0:T(8,128)(2,1)S(1)} %scatter_custom_fusion.3), channel_id=1, source_target_pairs={{0,2},{2,4},{4,6},{6,8},{8,10},{10,12},{12,14},{1,3},{3,5},{5,7},{... | collective-permute-start | bytes 1179656 | tf_op jit(solution)/shard_map/ppermute | solution.py:20
  144.3 1.4 copy-start.1
  150.5 13.8 %collective-permute-start.7 = (bf16[256,768]{1,0:T(8,128)(2,1)S(1)}, bf16[256,768]{1,0:T(8,128)(2,1)S(1)}, u32[]{:S(2)}, u32[]{:S(2)}) collective-permute-start(bf16[256,768]{1,0:T(8,128)(2,1)S(1)} %collective-permute-done.3), channel_id=1, source_target_pairs={{2,0},{4,2},{6,4},{8,6},{10,8},{12,10},{14,12},{3,1},{5,3},{7,5},{... | collective-permute-start | bytes 1179656 | tf_op jit(solution)/shard_map/ppermute | solution.py:20
  159.1 19.6 %collective-permute-start.5 = (bf16[256,768]{1,0:T(8,128)(2,1)S(1)}, bf16[256,768]{1,0:T(8,128)(2,1)S(1)}, u32[]{:S(2)}, u32[]{:S(2)}) collective-permute-start(bf16[256,768]{1,0:T(8,128)(2,1)S(1)} %collective-permute-done.1), channel_id=1, source_target_pairs={{0,2},{2,4},{4,6},{6,8},{8,10},{10,12},{12,14},{1,3},{3,5},{5,7},{... | collective-permute-start | bytes 1179656 | tf_op jit(solution)/shard_map/ppermute | solution.py:20
  163.9 14.8 %copy-start.6 = (pred[512]{0:T(512)(128)(4,1)S(1)}, pred[512]{0:T(512)(128)(4,1)}, u32[]{:S(2)}) copy-start(pred[512]{0:T(512)(128)(4,1)} %broadcast_compare_fusion.1) | copy-start | bytes 1540
  180.7 12.8 %all-to-all-start.2 = ((f32[8,1,64]{2,1,0:T(1,128)}), f32[8,1,64]{2,1,0:T(1,128)S(1)}, u32[]{:S(2)}, u32[]{:S(2)}) async-start(f32[8,1,64]{2,1,0:T(1,128)} %max.65), calls=%async_computation.2 | async-start | bytes 8192 | tf_op jit(solution)/shard_map/all_to_all | solution.py:111
Sparse Core Ops, SparseCore 0:
  24.9 19.7 all-reduce.2
  48.1 72.9 all-reduce.4
  122.7 8.8 all-gather.2
